TPU v7x, 32 devices: a whole 2x2x4 slice. The times are simulated.
32 devices in a mesh: replica: 2 (over core), dp: 16 (over z, y, x).
Axes of the slice: x: 2, y: 2, z: 4, core: 2. Of those that a mesh axis runs over, the one named last changes fastest.
Arguments:
- layer_input: bfloat16 [2, 6144, 3072], P('replica', 'dp'), may hold values from -6 to 6
- key_cotangent: bfloat16 [2, 6144, 512], P('replica', 'dp'), may hold values from -0.029907227 to 0.029907227
- local_params: float32 [2, 3072, 512], P('replica', 'dp'), may hold values from -6 to 6
- global_params: float32 [3072, 512], P('dp'), may hold values from -6 to 6
- outer_momentum: float32 [16, 192, 512], P('dp', 'replica'), may hold values from -3 to 3
- adam_first: float32 [2, 3072, 512], P('replica', 'dp'), may hold values from -2 to 2
- adam_second: float32 [2, 3072, 512], P('replica', 'dp'), may hold values from 0.25 to 4
Outputs:
- merged_params: bfloat16 [2, 3072, 512], P('replica')
- new_global: float32 [3072, 512], P('dp')
- new_momentum: float32 [16, 192, 512], P('dp', 'replica')
- new_first: float32 [2, 3072, 512], P('replica', 'dp')
- new_second: float32 [2, 3072, 512], P('replica', 'dp')
All inputs are finite; a program needn't handle non-finite values.
Results may differ from a plain program's by a relative error of at most 0.0004.
Values may be sent and summed in bfloat16 or wider, within the bound.
A program may use at most 64 MiB of HBM per device.

v0:
```python
import jax
import jax.numpy as jnp
from jax import lax
from jax.sharding import PartitionSpec as P

outer_mu = 0.9
outer_rate = 0.7
beta_one = 0.9
beta_two = 0.95
adam_eps = 1e-08
weight_decay = 0.1
inner_rate = 0.1
correct_one = 1.0 - 0.9**50
correct_two = 1.0 - 0.95**50


def per_device(
    layer_input, key_cotangent, local_params, global_params, outer_momentum, adam_first, adam_second
):
    features = layer_input[0]
    cotangent = key_cotangent[0]
    own_local = local_params[0]
    whole_term = lax.dot_general(
        features, cotangent, (((0,), (0,)), ((), ())), preferred_element_type=jnp.float32
    )
    gradient = lax.psum_scatter(whole_term, "dp", scatter_dimension=0, tiled=True)
    replicas = lax.axis_size("replica")
    deltas = global_params - own_local
    sub_rows = outer_momentum.shape[1]
    row_offset = lax.axis_index("replica") * sub_rows
    old_rows = lax.all_gather(outer_momentum[0], "replica", axis=0, tiled=True)
    outer_grad = lax.psum(deltas, "replica") / replicas
    momentum_all = outer_mu * old_rows + outer_grad
    global_new = global_params - outer_rate * (outer_grad + outer_mu * momentum_all)
    momentum_new = lax.dynamic_slice_in_dim(momentum_all, row_offset, sub_rows, 0)
    first_new = beta_one * adam_first[0] + (1.0 - beta_one) * gradient
    second_new = beta_two * adam_second[0] + (1.0 - beta_two) * gradient * gradient
    adam_step = (
        first_new / correct_one / (jnp.sqrt(second_new / correct_two) + adam_eps)
        + weight_decay * own_local
    )
    merged_rows = (global_new - inner_rate * adam_step).astype(jnp.bfloat16)
    gathered = lax.all_gather(merged_rows, "dp", axis=0, tiled=True)
    return (gathered[None], global_new, momentum_new[None], first_new[None], second_new[None])


def solution(mesh):
    placed = (
        P("replica", "dp", None),
        P("replica", "dp", None),
        P("replica", "dp", None),
        P("dp", None),
        P("dp", "replica", None),
        P("replica", "dp", None),
        P("replica", "dp", None),
    )
    return jax.shard_map(
        per_device,
        mesh=mesh,
        in_specs=placed,
        out_specs=(
            P("replica", None, None),
            P("dp", None),
            P("dp", "replica", None),
            P("replica", "dp", None),
            P("replica", "dp", None),
        ),
        check_vma=False,
    )
```

profile of v0, /device:TPU:0, one launch (start us, length us, event | category | flops | bytes accessed | tf_op | source)
XLA Modules:
  0.0 246.8 jit_solution(10030431163327194916)
XLA Ops:
  8.0 0.0 copy-start
  8.0 0.0 all-reduce.2.cloned.1.call-start
  8.1 2.1 bitcast_subtract_fusion
  10.1 0.0 all-reduce.2.cloned.1.call-update
  10.1 0.0 reduce-scatter.2.cloned.1.call-start
  10.2 0.0 copy-done
  10.2 5.5 %fusion = f32[3072,512]{1,0:T(8,128)} fusion(bf16[1,384,3072]{2,1,0:T(8,128)(2,1)S(1)} %copy-done, bf16[1,384,512]{2,1,0:T(8,128)(2,1)} %param.8), kind=kOutput, calls=%fused_computation | convolution fusion | flops 1207959552 | bytes 9043968 | tf_op jit(solution)/shard_map/dot_general | solution.py:23
  15.7 0.0 copy-start.1
  15.7 0.0 copy-start.2
  15.7 0.0 reduce-scatter.2.cloned.1.call-update
  15.7 0.0 all-gather.3.cloned.1.call-start
  15.8 2.6 %all-gather = f32[1,192,512]{2,1,0:T(8,128)S(1)} all-gather(f32[1,96,512]{2,1,0:T(8,128)} %param.11), channel_id=2, replica_groups=mesh['replica'=2,'dp'=16] {'replica'}, dimensions={1}, use_global_device_ids=true | all-gather | bytes 589824 | tf_op jit(solution)/shard_map/all_gather | solution.py:31
  18.3 14.6 %all-reduce.2.cloned.1.call-done = f32[192,512]{1,0:T(8,128)} async-done(((f32[192,512]{1,0:T(8,128)}), f32[192,512]{1,0:T(8,128)}) %all-reduce.2.cloned.1.call-update) | async-done | bytes 393232 | tf_op jit(solution)/shard_map/psum | solution.py:32
  32.9 133.2 %reduce-scatter.2.cloned.1.call-done = f32[192,512]{1,0:T(8,128)} async-done(((f32[3072,512]{1,0:T(8,128)}), f32[192,512]{1,0:T(8,128)}) %reduce-scatter.2.cloned.1.call-update) | async-done | bytes 393232 | tf_op jit(solution)/shard_map/reduce_scatter | solution.py:26
  166.1 0.0 copy-done.1
  166.1 0.0 copy-done.2
  166.1 2.7 %fusion.7 = (bf16[192,512]{1,0:T(8,128)(2,1)}, f32[192,512]{1,0:T(8,128)}, f32[1,192,512]{2,1,0:T(8,128)}, f32[192,512]{1,0:T(8,128)}, f32[1,192,512]{2,1,0:T(8,128)}) fusion(f32[1,192,512]{2,1,0:T(8,128)S(1)} %copy-done.1, f32[192,512]{1,0:T(8,128)} %reduce-scatter.2.cloned.1.call-done, f32[1,192,512]{2,1,0:T(8,128)} %param.12, f32[1,192,512]{2,1,0:T(8,128)} %param.13, ...), kind=kLoop, calls=%fused_computation.12 | loop fusion | flops 2260992 | bytes 4521984 | tf_op jit(solution)/shard_map/convert_element_type | solution.py:42
  168.8 0.0 all-gather.3.cloned.1.call-update
  168.8 1.6 dynamic-slice_bitcast_fusion
  170.4 65.1 %all-gather.3.cloned.1.call-done = bf16[3072,512]{1,0:T(8,128)(2,1)} async-done(((bf16[192,512]{1,0:T(8,128)(2,1)}), bf16[3072,512]{1,0:T(8,128)(2,1)}) %all-gather.3.cloned.1.call-update) | async-done | bytes 3145744 | tf_op jit(solution)/shard_map/all_gather | solution.py:43
  235.6 3.8 %copy.14 = bf16[1,3072,512]{2,1,0:T(8,128)(2,1)} copy(bf16[1,3072,512]{2,1,0:T(8,128)(2,1)} %bitcast.41) | data formatting | bytes 6291456
Async XLA Ops:
  8.0 2.2 copy-start
  8.0 24.9 %all-reduce.2.cloned.1.call-start = ((), (), s32[]{:S(2)}) async-start(), calls=%async_computation.1 | async-start | bytes 786432 | tf_op jit(solution)/shard_map/psum | solution.py:32
  10.1 155.9 %reduce-scatter.2.cloned.1.call-start = ((), (), s32[]{:S(2)}) async-start(), calls=%async_computation.2 | async-start | bytes 6684672 | tf_op jit(solution)/shard_map/reduce_scatter | solution.py:26
  15.7 150.4 %copy-start.1 = (f32[1,192,512]{2,1,0:T(8,128)S(1)}, f32[1,192,512]{2,1,0:T(8,128)}, u32[]{:S(2)}) copy-start(f32[1,192,512]{2,1,0:T(8,128)} %param.9) | copy-start | bytes 1179652
  15.7 150.4 %copy-start.2 = (f32[192,512]{1,0:T(8,128)S(1)}, f32[192,512]{1,0:T(8,128)}, u32[]{:S(2)}) copy-start(f32[192,512]{1,0:T(8,128)} %param.10) | copy-start | bytes 1179652
  15.7 219.8 %all-gather.3.cloned.1.call-start = ((), (), s32[]{:S(2)}) async-start(), calls=%async_computation.3 | async-start | bytes 3342336 | tf_op jit(solution)/shard_map/all_gather | solution.py:43
Sparse Core Ops, SparseCore 0:
  11.7 21.1 all-reduce.1
Sparse Core Ops, SparseCore 1:
  15.9 150.2 reduce-scatter.1
  168.9 66.6 all-gather.2
where the time goes:
time: 247 us
  waiting for transfers between devices  213 us (86%)
  between operations  15.5 us (6%)
  matrix products  5.49 us (2%)
  local copies, waits for them, and re-layouts  5.39 us (2%)
  other arithmetic  4.75 us (2%)
  blocking collectives  2.55 us (1%)
    reduce_scatter x1, waiting for transfers between devices, per_device(): lax.psum_scatter(whole_term, 'dp', scatter_dimension=0, tiled=True)  133 us
    all_gather x1, waiting for transfers between devices, per_device(): gathered = lax.all_gather(merged_rows, 'dp', axis=0, tiled=True)  65.1 us
    psum x1, waiting for transfers between devices, per_device(): outer_grad = lax.psum(deltas, 'replica') / replicas  14.6 us
    dot_general x1, matrix products, per_device(): lax.dot_general(features, cotangent, (((0,), (0,)), ((), ())), preferred_...  5.49 us
  transfers between devices with their start and end apart: 3, of which 3 were waited for; matrix products, arithmetic and copies ran while one was open for 3% of the time, Pallas kernels for 0%

commit v1 on v0

v1 whole, which is shorter than its diff:
```python
import functools
import jax
import jax.numpy as jnp
from jax import lax
from jax.experimental import pallas as pl
from jax.experimental.pallas import tpu as pltpu
from jax.sharding import PartitionSpec as P

outer_mu = 0.9
outer_rate = 0.7
beta_one = 0.9
beta_two = 0.95
adam_eps = 1e-08
weight_decay = 0.1
inner_rate = 0.1
correct_one = 1.0 - 0.9**50
correct_two = 1.0 - 0.95**50

MESH = pl.DeviceIdType.MESH
HALVES = 2
NARROW_STAGES = 1


def bit_of(value, bit):
    return lax.rem(lax.div(value, 2**bit), 2)


def flipped(value, bit):
    return value + (1 - 2 * bit_of(value, bit)) * 2**bit


def free_bits(bits, done):
    return [b for b in range(bits) if b not in done]


def owner_at(bits, me, done, flip, slot):
    owner = 0
    for position, b in enumerate(free_bits(bits, done)):
        owner = owner + bit_of(slot, position) * 2**b
    for b in done:
        own = bit_of(me, b)
        owner = owner + (1 - own if b == flip else own) * 2**b
    return owner


def slot_of(bits, done, owner):
    slot = 0
    for position, b in enumerate(free_bits(bits, done)):
        slot = slot + bit_of(owner, b) * 2**position
    return slot


def place_of(order, owner):
    place = 0
    for position, b in enumerate(reversed(order)):
        place = place + bit_of(owner, b) * 2**position
    return place


def static_place(order, owner):
    return sum(((owner >> b) & 1) << position for position, b in enumerate(reversed(order)))


def orders_of(bits):
    rising = list(range(bits))
    swapped = rising[:2][::-1] + rising[2:]
    return [rising, swapped]


def kernel(
    n_dp, n_rep, splits, x_ref, c_ref, local_ref, global_ref, mom_ref, first_ref, second_ref,
    merged_ref, gnew_ref, mnew_ref, fnew_ref, snew_ref,
    grad, deltas, moms, mom_flat, outer, gathered, *rest,
):
    bits = n_dp.bit_length() - 1
    sends, recvs = rest[:bits], rest[bits:2 * bits]
    send_sem, recv_sem, gsend_sem, grecv_sem, rep_send, rep_recv, out_sem = rest[2 * bits:]
    rep, me = lax.axis_index("replica"), lax.axis_index("dp")
    rows0, width = local_ref.shape
    rows, cols = rows0 // splits, width // HALVES
    sub = mom_ref.shape[0]
    orders = orders_of(bits)

    barrier = pltpu.get_barrier_semaphore()
    for b in range(bits):
        pl.semaphore_signal(barrier, inc=1, device_id=(rep, flipped(me, b)), device_id_type=MESH)
    for d in range(1, n_rep):
        pl.semaphore_signal(
            barrier, inc=1, device_id=(lax.rem(rep + d, n_rep), me), device_id_type=MESH
        )
    pl.semaphore_wait(barrier, bits + n_rep - 1)

    rep_copies = []
    for d in range(1, n_rep):
        target = (lax.rem(rep + d, n_rep), me)
        for which, (src, dst) in enumerate(((local_ref, deltas), (mom_ref, moms))):
            copy = pltpu.make_async_remote_copy(
                src_ref=src, dst_ref=dst.at[d], send_sem=rep_send.at[d, which],
                recv_sem=rep_recv.at[d, which], device_id=target, device_id_type=MESH,
            )
            copy.start()
            rep_copies.append(copy)

    block = 128

    def product(i, carry):
        at = pl.ds(pl.multiple_of(i * block, block), block)
        grad[at, :] = lax.dot_general(
            x_ref[:, at], c_ref[...], (((0,), (0,)), ((), ())),
            preferred_element_type=jnp.float32,
        )
        return carry

    lax.fori_loop(0, x_ref.shape[1] // block, product, 0)

    def rows_of(owner, q):
        return pl.ds(pl.multiple_of(owner * rows0 + q * rows, 8), rows)

    def update_outer():
        for copy in rep_copies:
            copy.wait()
        moms[0] = mom_ref[...]
        deltas[0] = local_ref[...]
        for r in range(n_rep):
            mom_flat[r * sub:(r + 1) * sub, :] = moms[lax.rem(rep - r + n_rep, n_rep)]
        total = jnp.zeros(local_ref.shape, jnp.float32)
        for r in range(n_rep):
            total = total + (global_ref[...] - deltas[lax.rem(rep - r + n_rep, n_rep)])
        outer_grad = total / n_rep
        momentum = outer_mu * mom_flat[...] + outer_grad
        outer[...] = momentum
        gnew_ref[...] = global_ref[...] - outer_rate * (outer_grad + outer_mu * momentum)
        for r in range(n_rep):
            @pl.when(rep == r)
            def _():
                mnew_ref[...] = outer[r * sub:(r + 1) * sub, :]

    def steps(q, h):
        order = orders[h]
        ch = q * HALVES + h
        lanes = slice(h * cols, (h + 1) * cols)

        def halving(stage):
            b = order[stage]
            return pltpu.make_async_remote_copy(
                src_ref=sends[stage].at[ch], dst_ref=recvs[stage].at[ch],
                send_sem=send_sem.at[ch, stage], recv_sem=recv_sem.at[ch, stage],
                device_id=(rep, flipped(me, b)), device_id_type=MESH,
            )

        for stage in range(bits):
            done = order[:stage + 1]
            count = n_dp >> (stage + 1)
            b = order[stage]
            if stage:
                halving(stage - 1).wait()

            def fill(slot, carry):
                owner = owner_at(bits, me, done, b, slot)
                value = grad[rows_of(owner, q), lanes]
                if stage:
                    arrived = slot_of(bits, order[:stage], owner)
                    value = value + recvs[stage - 1][ch, arrived].astype(jnp.float32)
                sends[stage][ch, slot] = value.astype(sends[stage].dtype)
                return carry

            lax.fori_loop(0, count, fill, 0)
            halving(stage).start()

            if stage:
                def keep(slot, carry):
                    owner = owner_at(bits, me, done, None, slot)
                    arrived = slot_of(bits, order[:stage], owner)
                    at = rows_of(owner, q)
                    grad[at, lanes] = grad[at, lanes] + recvs[stage - 1][ch, arrived].astype(
                        jnp.float32
                    )
                    return carry

                lax.fori_loop(0, count, keep, 0)
            yield

        halving(bits - 1).wait()
        own = slice(q * rows, (q + 1) * rows)
        gradient = grad[rows_of(me, q), lanes] + recvs[bits - 1][ch, 0].astype(jnp.float32)
        first_new = beta_one * first_ref[own, lanes] + (1.0 - beta_one) * gradient
        second_new = beta_two * second_ref[own, lanes] + (1.0 - beta_two) * gradient * gradient
        fnew_ref[own, lanes] = first_new
        snew_ref[own, lanes] = second_new
        adam_step = (
            first_new / correct_one / (jnp.sqrt(second_new / correct_two) + adam_eps)
            + weight_decay * local_ref[own, lanes]
        )
        mine = place_of(order, me)
        gathered[ch, mine] = (gnew_ref[own, lanes] - inner_rate * adam_step).astype(jnp.bfloat16)

        for stage in range(bits):
            b = order[bits - 1 - stage]
            if stage:
                copy.wait()
            held = gathered.at[ch, pl.ds(lax.div(mine, 2**stage) * 2**stage, 2**stage)]
            copy = pltpu.make_async_remote_copy(
                src_ref=held, dst_ref=held,
                send_sem=gsend_sem.at[ch, stage], recv_sem=grecv_sem.at[ch, stage],
                device_id=(rep, flipped(me, b)), device_id_type=MESH,
            )
            copy.start()
            yield
        copy.wait()
        for owner in range(n_dp):
            pltpu.make_async_copy(
                gathered.at[ch, static_place(order, owner)],
                merged_ref.at[owner, own, lanes], out_sem.at[ch],
            ).start()
        yield

    chunks = [[steps(q, h) for h in range(HALVES)] for q in range(splits)]
    ticks = 2 * bits + 1
    for tick in range(ticks + splits - 1):
        first = [tick] if tick < splits else []
        for q in first + [q for q in range(splits) if q < tick and tick - q < ticks]:
            for chunk in chunks[q]:
                next(chunk)
        if tick == 0:
            update_outer()
    for q in range(splits):
        for h in range(HALVES):
            ch = q * HALVES + h
            pltpu.make_async_copy(
                gathered.at[ch],
                merged_ref.at[:, q * rows:(q + 1) * rows, h * cols:(h + 1) * cols],
                out_sem.at[ch],
            ).wait()


def per_device(
    layer_input, key_cotangent, local_params, global_params, outer_momentum, adam_first, adam_second
):
    n_dp, n_rep = lax.axis_size("dp"), lax.axis_size("replica")
    bits = n_dp.bit_length() - 1
    rows0, width = global_params.shape
    sub = outer_momentum.shape[1]
    features = layer_input.shape[2]
    splits = next(s for s in (4, 2, 1) if s == 1 or rows0 % (s * 16) == 0)
    channels = splits * HALVES
    rows, cols = rows0 // splits, width // HALVES
    f32 = jnp.float32

    def stage_buffers():
        return [
            pltpu.VMEM(
                (channels, n_dp >> (s + 1), rows, cols),
                jnp.bfloat16 if s < NARROW_STAGES else f32,
            )
            for s in range(bits)
        ]

    vmem = pl.BlockSpec(memory_space=pltpu.VMEM)
    merged, gnew, mnew, fnew, snew = pl.pallas_call(
        functools.partial(kernel, n_dp, n_rep, splits),
        out_shape=(
            jax.ShapeDtypeStruct((n_dp, rows0, width), jnp.bfloat16),
            jax.ShapeDtypeStruct((rows0, width), f32),
            jax.ShapeDtypeStruct((sub, width), f32),
            jax.ShapeDtypeStruct((rows0, width), f32),
            jax.ShapeDtypeStruct((rows0, width), f32),
        ),
        in_specs=[vmem] * 7,
        out_specs=(pl.BlockSpec(memory_space=pl.ANY),) + (vmem,) * 4,
        scratch_shapes=[
            pltpu.VMEM((features, width), f32),
            pltpu.VMEM((n_rep, rows0, width), f32),
            pltpu.VMEM((n_rep, sub, width), f32),
            pltpu.VMEM((rows0, width), f32),
            pltpu.VMEM((rows0, width), f32),
            pltpu.VMEM((channels, n_dp, rows, cols), jnp.bfloat16),
            *stage_buffers(),
            *stage_buffers(),
            pltpu.SemaphoreType.DMA((channels, bits)),
            pltpu.SemaphoreType.DMA((channels, bits)),
            pltpu.SemaphoreType.DMA((channels, bits)),
            pltpu.SemaphoreType.DMA((channels, bits)),
            pltpu.SemaphoreType.DMA((n_rep, 2)),
            pltpu.SemaphoreType.DMA((n_rep, 2)),
            pltpu.SemaphoreType.DMA((channels,)),
        ],
        compiler_params=pltpu.CompilerParams(
            collective_id=0, has_side_effects=True, vmem_limit_bytes=60 * 2**20
        ),
    )(
        layer_input[0], key_cotangent[0], local_params[0], global_params, outer_momentum[0],
        adam_first[0], adam_second[0],
    )
    return (merged.reshape(1, n_dp * rows0, width), gnew, mnew[None], fnew[None], snew[None])


def solution(mesh):
    placed = (
        P("replica", "dp", None),
        P("replica", "dp", None),
        P("replica", "dp", None),
        P("dp", None),
        P("dp", "replica", None),
        P("replica", "dp", None),
        P("replica", "dp", None),
    )
    return jax.shard_map(
        per_device,
        mesh=mesh,
        in_specs=placed,
        out_specs=(
            P("replica", None, None),
            P("dp", None),
            P("dp", "replica", None),
            P("replica", "dp", None),
            P("replica", "dp", None),
        ),
        check_vma=False,
    )
```

time: 247 us -> 104 us (0.42)
  waiting for transfers between devices: 213 us -> 0 us
  Pallas kernels: 0 us -> 96.4 us
  between operations: 15.5 us -> 0.68 us
  matrix products: 5.49 us -> 0 us
  other arithmetic: 4.75 us -> 0 us
  blocking collectives: 2.55 us -> 0 us
    reduce_scatter x1 -> x0, waiting for transfers between devices: 133 us -> none  [per_device(): lax.psum_scatter(whole_term, 'dp', scatter_dimension=0, tiled=True)]
    pallas_call x0 -> x1, Pallas kernels: none -> 96.4 us  [per_device(): pl.pallas_call(functools.partial(kernel, n_dp, n_rep, splits), out_shape=...]
    all_gather x1 -> x0, waiting for transfers between devices: 65.1 us -> none  [per_device(): gathered = lax.all_gather(merged_rows, 'dp', axis=0, tiled=True)]
    psum x1 -> x0, waiting for transfers between devices: 14.6 us -> none  [per_device(): outer_grad = lax.psum(deltas, 'replica') / replicas]
    dot_general x1 -> x0, matrix products: 5.49 us -> none  [per_device(): lax.dot_general(features, cotangent, (((0,), (0,)), ((), ())), preferred_...]
    unnamed x7 -> x13, local copies, waits for them, and re-layouts: 3.77 us -> 6.79 us
    convert_element_type x1 -> x0, other arithmetic: 2.69 us -> none  [per_device(): merged_rows = (global_new - inner_rate * adam_step).astype(jnp.bfloat16)]
    all_gather x1 -> x0, blocking collectives: 2.55 us -> none  [per_device(): old_rows = lax.all_gather(outer_momentum[0], 'replica', axis=0, tiled=True)]
  transfers between devices with their start and end apart: 3 -> 0, of which waited for: 3 -> 0; matrix products, arithmetic and copies ran while one was open for 3% -> 0% of each run, Pallas kernels for 0% -> 0%
where the time goes in v1:
time: 104 us
  Pallas kernels  96.4 us (93%)
  local copies, waits for them, and re-layouts  6.79 us (7%)
    pallas_call x1, Pallas kernels, per_device(): pl.pallas_call(functools.partial(kernel, n_dp, n_rep, splits), out_shape=...  96.4 us
    unnamed x13, local copies, waits for them, and re-layouts  6.79 us

profile of v1, /device:TPU:0, one launch (start us, length us, event | category | flops | bytes accessed | tf_op | source)
XLA Modules:
  0.0 103.8 jit_solution(11579833962698147986)
XLA Ops:
  0.6 96.4 %shard_map.110 = (bf16[16,192,512]{2,1,0:T(8,128)(2,1)}, f32[192,512]{1,0:T(8,128)}, f32[96,512]{1,0:T(8,128)}, f32[192,512]{1,0:T(8,128)}, f32[192,512]{1,0:T(8,128)}) custom-call(bf16[384,3072]{1,0:T(8,128)(2,1)} %bitcast.11, bf16[384,512]{1,0:T(8,128)(2,1)} %bitcast.12, f32[192,512]{1,0:T(8,128)} %bitcast.13, f32[192,512]{1,0:T(8,128)} %global_ref.1, ...), custom_call_target="tpu_custom_call" | custom-call | tf_op jit(solution)/shard_map/pallas_call | solution.py:259
  97.0 0.0 copy-start.2
  97.0 0.0 copy-start.3
  97.0 0.0 copy-start.1
  97.0 0.0 copy-start
  97.0 3.9 %copy.17 = bf16[1,3072,512]{2,1,0:T(8,128)(2,1)} copy(bf16[1,3072,512]{2,1,0:T(8,128)(2,1)} %bitcast.10) | data formatting | bytes 6291456
  100.9 0.0 copy-done.2
  100.9 0.7 copy.18
  101.6 0.0 copy-done.3
  101.6 0.7 copy.19
  102.3 0.0 copy-done.1
  102.3 0.7 copy.20
  103.1 0.0 copy-done
  103.1 0.7 copy.21
Async XLA Ops:
  97.0 3.9 %copy-start.2 = (f32[192,512]{1,0:T(8,128)S(1)}, f32[192,512]{1,0:T(8,128)}, u32[]{:S(2)}) copy-start(f32[192,512]{1,0:T(8,128)} %get-tuple-element.21) | copy-start | bytes 1179652
  97.0 4.6 %copy-start.3 = (f32[96,512]{1,0:T(8,128)S(1)}, f32[96,512]{1,0:T(8,128)}, u32[]{:S(2)}) copy-start(f32[96,512]{1,0:T(8,128)} %get-tuple-element.12) | copy-start | bytes 589828
  97.0 5.3 %copy-start.1 = (f32[192,512]{1,0:T(8,128)S(1)}, f32[192,512]{1,0:T(8,128)}, u32[]{:S(2)}) copy-start(f32[192,512]{1,0:T(8,128)} %get-tuple-element.13) | copy-start | bytes 1179652
  97.0 6.0 %copy-start = (f32[192,512]{1,0:T(8,128)S(1)}, f32[192,512]{1,0:T(8,128)}, u32[]{:S(2)}) copy-start(f32[192,512]{1,0:T(8,128)} %get-tuple-element.14) | copy-start | bytes 1179652

commit v2 on v1

--- a/solution.py
+++ b/solution.py
@@ -18,10 +18,19 @@
 
 MESH = pl.DeviceIdType.MESH
 HALVES = 2
-NARROW_STAGES = 1
+NARROW_STAGES = 3
+UNROLL = 8
+SPLITS = (12, 6, 4, 2, 1)
+LATE = ()
+START = 2
+STRIDE = 4
+OUTER_AFTER = 1
+BLOCK = 1024
 
 
 def bit_of(value, bit):
+    if isinstance(value, int):
+        return (value >> bit) & 1
     return lax.rem(lax.div(value, 2**bit), 2)
 
 
@@ -34,20 +43,24 @@
 
 
 def owner_at(bits, me, done, flip, slot):
-    owner = 0
-    for position, b in enumerate(free_bits(bits, done)):
-        owner = owner + bit_of(slot, position) * 2**b
+    fixed = 0
     for b in done:
         own = bit_of(me, b)
-        owner = owner + (1 - own if b == flip else own) * 2**b
-    return owner
-
-
-def slot_of(bits, done, owner):
-    slot = 0
+        fixed = fixed + (1 - own if b == flip else own) * 2**b
+    spread = 0
     for position, b in enumerate(free_bits(bits, done)):
-        slot = slot + bit_of(owner, b) * 2**position
-    return slot
+        spread = spread + bit_of(slot, position) * 2**b
+    return fixed + spread
+
+
+def arrival_of(bits, done, last, slot):
+    position = free_bits(bits, done[:-1]).index(done[-1])
+    if isinstance(slot, int):
+        above = slot >> position
+    else:
+        above = lax.div(slot, 2**position)
+    below = slot - above * 2**position
+    return above * 2 ** (position + 1) + below + last * 2**position
 
 
 def place_of(order, owner):
@@ -61,10 +74,20 @@
     return sum(((owner >> b) & 1) << position for position, b in enumerate(reversed(order)))
 
 
-def orders_of(bits):
+def orders_of(bits, late):
     rising = list(range(bits))
-    swapped = rising[:2][::-1] + rising[2:]
-    return [rising, swapped]
+    low, high = rising[:2], rising[2:]
+    if late:
+        return [high + low, high + low[::-1]]
+    return [low + high, low[::-1] + high]
+
+
+def for_slots(count, body):
+    if count <= UNROLL:
+        for slot in range(count):
+            body(slot)
+    else:
+        lax.fori_loop(0, count, lambda slot, carry: (body(slot), carry)[1], 0)
 
 
 def kernel(
@@ -79,7 +102,6 @@
     rows0, width = local_ref.shape
     rows, cols = rows0 // splits, width // HALVES
     sub = mom_ref.shape[0]
-    orders = orders_of(bits)
 
     barrier = pltpu.get_barrier_semaphore()
     for b in range(bits):
@@ -101,7 +123,7 @@
             copy.start()
             rep_copies.append(copy)
 
-    block = 128
+    block = BLOCK
 
     def product(i, carry):
         at = pl.ds(pl.multiple_of(i * block, block), block)
@@ -136,7 +158,7 @@
                 mnew_ref[...] = outer[r * sub:(r + 1) * sub, :]
 
     def steps(q, h):
-        order = orders[h]
+        order = orders_of(bits, q in LATE)[h]
         ch = q * HALVES + h
         lanes = slice(h * cols, (h + 1) * cols)
 
@@ -155,29 +177,27 @@
             if stage:
                 halving(stage - 1).wait()
 
-            def fill(slot, carry):
+            def fill(slot):
                 owner = owner_at(bits, me, done, b, slot)
                 value = grad[rows_of(owner, q), lanes]
                 if stage:
-                    arrived = slot_of(bits, order[:stage], owner)
+                    arrived = arrival_of(bits, done, 1 - bit_of(me, b), slot)
                     value = value + recvs[stage - 1][ch, arrived].astype(jnp.float32)
                 sends[stage][ch, slot] = value.astype(sends[stage].dtype)
-                return carry
-
-            lax.fori_loop(0, count, fill, 0)
+
+            for_slots(count, fill)
             halving(stage).start()
 
             if stage:
-                def keep(slot, carry):
+                def keep(slot):
                     owner = owner_at(bits, me, done, None, slot)
-                    arrived = slot_of(bits, order[:stage], owner)
+                    arrived = arrival_of(bits, done, bit_of(me, b), slot)
                     at = rows_of(owner, q)
                     grad[at, lanes] = grad[at, lanes] + recvs[stage - 1][ch, arrived].astype(
                         jnp.float32
                     )
-                    return carry
-
-                lax.fori_loop(0, count, keep, 0)
+
+                for_slots(count, keep)
             yield
 
         halving(bits - 1).wait()
@@ -215,13 +235,13 @@
         yield
 
     chunks = [[steps(q, h) for h in range(HALVES)] for q in range(splits)]
-    ticks = 2 * bits + 1
-    for tick in range(ticks + splits - 1):
-        first = [tick] if tick < splits else []
-        for q in first + [q for q in range(splits) if q < tick and tick - q < ticks]:
-            for chunk in chunks[q]:
-                next(chunk)
-        if tick == 0:
+    due = sorted(
+        (START * q + STRIDE * i, i > 0, q) for q in range(splits) for i in range(2 * bits + 1)
+    )
+    for count, (_, _, q) in enumerate(due):
+        for chunk in chunks[q]:
+            next(chunk)
+        if count == OUTER_AFTER:
             update_outer()
     for q in range(splits):
         for h in range(HALVES):
@@ -233,6 +253,44 @@
             ).wait()
 
 
+def finish_kernel(parts, *refs):
+    count = len(parts)
+    sources, results, held = refs[:count], refs[count:2 * count], refs[2 * count:3 * count]
+    sem = refs[3 * count]
+    pieces = []
+    for index, cuts in enumerate(parts):
+        size = sources[index].shape[0] // cuts
+        for cut in range(cuts):
+            pieces.append((index, slice(cut * size, (cut + 1) * size)))
+    ins = [
+        pltpu.make_async_copy(sources[i].at[at], held[i].at[at], sem.at[0, p])
+        for p, (i, at) in enumerate(pieces)
+    ]
+    outs = [
+        pltpu.make_async_copy(held[i].at[at], results[i].at[at], sem.at[1, p])
+        for p, (i, at) in enumerate(pieces)
+    ]
+    for copy in ins:
+        copy.start()
+    for copy, onward in zip(ins, outs):
+        copy.wait()
+        onward.start()
+    for copy in outs:
+        copy.wait()
+
+
+def finish(*arrays):
+    parts = [8 if a.ndim == 3 and a.shape[0] % 8 == 0 else 1 for a in arrays]
+    return pl.pallas_call(
+        functools.partial(finish_kernel, parts),
+        out_shape=tuple(jax.ShapeDtypeStruct(a.shape, a.dtype) for a in arrays),
+        in_specs=[pl.BlockSpec(memory_space=pl.ANY)] * len(arrays),
+        out_specs=tuple([pl.BlockSpec(memory_space=pl.ANY)] * len(arrays)),
+        scratch_shapes=[pltpu.VMEM(a.shape, a.dtype) for a in arrays]
+        + [pltpu.SemaphoreType.DMA((2, sum(parts)))],
+    )(*arrays)
+
+
 def per_device(
     layer_input, key_cotangent, local_params, global_params, outer_momentum, adam_first, adam_second
 ):
@@ -241,7 +299,7 @@
     rows0, width = global_params.shape
     sub = outer_momentum.shape[1]
     features = layer_input.shape[2]
-    splits = next(s for s in (4, 2, 1) if s == 1 or rows0 % (s * 16) == 0)
+    splits = next(s for s in SPLITS if s == 1 or rows0 % (s * 16) == 0)
     channels = splits * HALVES
     rows, cols = rows0 // splits, width // HALVES
     f32 = jnp.float32
@@ -256,7 +314,7 @@
         ]
 
     vmem = pl.BlockSpec(memory_space=pltpu.VMEM)
-    merged, gnew, mnew, fnew, snew = pl.pallas_call(
+    results = pl.pallas_call(
         functools.partial(kernel, n_dp, n_rep, splits),
         out_shape=(
             jax.ShapeDtypeStruct((n_dp, rows0, width), jnp.bfloat16),
@@ -291,6 +349,7 @@
         layer_input[0], key_cotangent[0], local_params[0], global_params, outer_momentum[0],
         adam_first[0], adam_second[0],
     )
+    merged, gnew, mnew, fnew, snew = finish(*results)
     return (merged.reshape(1, n_dp * rows0, width), gnew, mnew[None], fnew[None], snew[None])
 
 

time: 104 us -> 75.6 us (0.73)
  Pallas kernels: 96.4 us -> 74.8 us
  local copies, waits for them, and re-layouts: 6.79 us -> 0 us
    pallas_call x1, Pallas kernels: 96.4 us -> 70.8 us  [per_device(): pl.pallas_call(functools.partial(kernel, n_dp, n_rep, splits), out_shape=...]
    unnamed x13 -> x0, local copies, waits for them, and re-layouts: 6.79 us -> none
    pallas_call x0 -> x1, Pallas kernels: none -> 4.05 us  [finish(): pl.pallas_call(functools.partial(finish_kernel, parts), out_shape=tuple((...]
where the time goes in v2:
time: 75.6 us; the launch traced here: 75.5 us
  Pallas kernels  74.8 us (99%)
    pallas_call x1, Pallas kernels, per_device(): pl.pallas_call(functools.partial(kernel, n_dp, n_rep, splits), out_shape=...  70.8 us
    pallas_call x1, Pallas kernels, finish(): pl.pallas_call(functools.partial(finish_kernel, parts), out_shape=tuple((...  4.05 us

profile of v2, /device:TPU:0, one launch (start us, length us, event | category | flops | bytes accessed | tf_op | source)
XLA Modules:
  0.0 75.5 jit_solution(11513770584146997970)
XLA Ops:
  0.6 70.8 %shard_map.110 = (bf16[16,192,512]{2,1,0:T(8,128)(2,1)}, f32[192,512]{1,0:T(8,128)}, f32[96,512]{1,0:T(8,128)}, f32[192,512]{1,0:T(8,128)}, f32[192,512]{1,0:T(8,128)}) custom-call(bf16[384,3072]{1,0:T(8,128)(2,1)} %bitcast.10, bf16[384,512]{1,0:T(8,128)(2,1)} %bitcast.11, f32[192,512]{1,0:T(8,128)} %bitcast.12, f32[192,512]{1,0:T(8,128)} %global_ref.1, ...), custom_call_target="tpu_custom_call" | custom-call | tf_op jit(solution)/shard_map/pallas_call | solution.py:317
  71.4 4.1 %shard_map.111 = (bf16[16,192,512]{2,1,0:T(8,128)(2,1)}, f32[192,512]{1,0:T(8,128)}, f32[96,512]{1,0:T(8,128)}, f32[192,512]{1,0:T(8,128)}, f32[192,512]{1,0:T(8,128)}) custom-call(bf16[16,192,512]{2,1,0:T(8,128)(2,1)} %get-tuple-element.15.refs_0_, f32[192,512]{1,0:T(8,128)} %get-tuple-element.16.refs_1_, f32[96,512]{1,0:T(8,128)} %get-tuple-element.17.refs_2_, ...), custom_call_target="tpu_custom_call" | custom-call | tf_op jit(solution)/shard_map/pallas_call | solution.py:284
